TPU v7x, 32 devices: a whole 2x2x4 slice. The times are simulated.
32 devices in a mesh: row: 4 (over x, core), col: 8 (over z, y).
Axes of the slice: x: 2, y: 2, z: 4, core: 2. Of those that a mesh axis runs over, the one named last changes fastest.
Arguments:
- points: float32 [16, 8192], P(None, ('row', 'col')), may hold values from -6 to 6
- lengthscale: float32 [16], replicated, may hold values from 2 to 8
- signal: float32 [1], replicated, may hold values from 0.5 to 2
- noise: float32 [1], replicated, may hold values from 0.05 to 0.5
- targets: float32 [8192], P(('row', 'col')), may hold values from -12 to 12
- probe_bits: int32 [31, 8192], P(None, ('row', 'col')), may hold values from 0 to 1
Outputs:
- solution: float32 [32, 8192], P(None, ('row', 'col'))
- residual: float32 [32, 8192], P(None, ('row', 'col'))
All inputs are finite; a program needn't handle non-finite values.
Results may differ from a plain program's by a relative error of at most 0.0013.
Values sent between devices are 32-bit elements; how exact they have to be, the bound alone decides.
No kernel may reach another device: no remote copies, remote signals or barrier semaphores. Data moves between devices by JAX's collectives and lax.ppermute only.
A program may use at most 128 MiB of HBM per device.

v0:
```python
import jax
import jax.numpy as jnp
from jax import lax
from jax.sharding import PartitionSpec as P

ITERS = 3
ROOT_FIVE = 5.0**0.5


def matern_tile(row_scaled, col_scaled, signal_value):
    row_sq = jnp.sum(row_scaled * row_scaled, axis=0)
    col_sq = jnp.sum(col_scaled * col_scaled, axis=0)
    cross_term = lax.dot_general(
        row_scaled,
        col_scaled,
        (((0,), (0,)), ((), ())),
        precision=lax.Precision.HIGHEST,
        preferred_element_type=jnp.float32,
    )
    dist_sq = jnp.maximum(row_sq[:, None] + col_sq[None, :] - 2.0 * cross_term, 0.0)
    radius = jnp.sqrt(dist_sq)
    return (
        signal_value
        * (1.0 + ROOT_FIVE * radius + 5.0 / 3.0 * dist_sq)
        * jnp.exp(-ROOT_FIVE * radius)
    )


def row_blocks(row_scaled):
    row_total = row_scaled.shape[1]
    block_rows = min(1024, row_total)
    block_count = row_total // block_rows
    return row_scaled.reshape(row_scaled.shape[0], block_count, block_rows).transpose(1, 0, 2)


def apply_tile(row_scaled, col_scaled, signal_value, vectors):
    row_total = row_scaled.shape[1]
    stacked = row_blocks(row_scaled)

    def one_block(row_block):
        kernel_tile = matern_tile(row_block, col_scaled, signal_value)
        return lax.dot_general(
            vectors,
            kernel_tile,
            (((1,), (1,)), ((), ())),
            precision=lax.Precision.HIGHEST,
            preferred_element_type=jnp.float32,
        )

    pieces = lax.map(one_block, stacked)
    return pieces.transpose(1, 0, 2).reshape(vectors.shape[0], row_total)


def squares(residual):
    return lax.psum(jnp.sum(residual * residual, axis=1), ("row", "col"))


def body(points, lengthscale, signal, noise, targets, probe_bits):
    scaled = points / lengthscale[:, None]
    signs = 2.0 * probe_bits.astype(jnp.float32) - 1.0
    right_side = jnp.concatenate([targets[None, :], signs], axis=0)
    signal_value = signal[0]
    noise_value = noise[0]
    every_point = lax.all_gather(scaled, ("row", "col"), axis=1, tiled=True)
    solution = jnp.zeros_like(right_side)
    residual = right_side
    direction = right_side
    norm_now = squares(residual)
    for step in range(ITERS):
        summed = apply_tile(
            scaled,
            every_point,
            signal_value,
            lax.all_gather(direction, ("row", "col"), axis=1, tiled=True),
        )
        image = summed + noise_value * direction
        curved = lax.psum(jnp.sum(direction * image, axis=1), ("row", "col"))
        alpha = norm_now / curved
        solution = solution + alpha[:, None] * direction
        residual = residual - alpha[:, None] * image
        if step + 1 < ITERS:
            norm_next = squares(residual)
            direction = residual + (norm_next / norm_now)[:, None] * direction
            norm_now = norm_next
    return (solution, residual)


def solution(mesh):
    return jax.shard_map(
        body,
        mesh=mesh,
        in_specs=(
            P(None, ("row", "col")),
            P(),
            P(),
            P(),
            P(("row", "col")),
            P(None, ("row", "col")),
        ),
        out_specs=(P(None, ("row", "col")), P(None, ("row", "col"))),
        check_vma=False,
    )
```

profile of v0, /device:TPU:0, one launch (start us, length us, event | category | flops | bytes accessed | tf_op | source)
XLA Modules:
  0.0 442.8 jit_solution(3945853298160864915)
XLA Ops:
  7.2 0.0 all-gather.4.cloned.1.call-start
  7.2 0.8 multiply_add_fusion.3
  8.0 1.3 pad_maximum_fusion
  9.3 0.0 all-gather.6.cloned.1.call-start
  10.6 0.8 multiply_reduce_fusion.7
  11.5 73.2 %all_gather.13 = f32[16,8192]{1,0:T(8,128)S(1)} all-gather(f32[16,256]{1,0:T(8,128)S(1)} %get-tuple-element.51), channel_id=1, replica_groups=mesh['row'=4,'col'=8] {'row','col'}, dimensions={1}, use_global_device_ids=true | all-gather | bytes 540672 | tf_op jit(solution)/shard_map/all_gather | solution.py:64
  84.6 0.1 multiply_reduce_fusion
  84.7 14.0 %exponential_multiply_fusion = f32[256,8192]{1,0:T(8,128)} fusion(f32[16,256]{1,0:T(8,128)S(1)} %get-tuple-element.51, f32[16,8192]{1,0:T(8,128)S(1)} %all_gather.13, f32[8192]{0:T(1024)S(1)} %multiply_reduce_fusion, f32[256]{0:T(256)S(1)} %get-tuple-element.50, f32[]{:T(128)} %bitcast.11), kind=kOutput, calls=%fused_computation.3 | convolution fusion | flops 425721856 | bytes 8963076 | tf_op jit(solution)/shard_map/while/body/eval_jaxpr/dot_general | solution.py:13
  98.8 11.2 %multiply_reduce_fusion.5 = (f32[32]{0:T(128)S(1)}, f32[32]{0:T(128)S(1)}, f32[32,256]{1,0:T(8,128)S(1)}) fusion(f32[32,256]{1,0:T(8,128)S(1)} %copy-done.2, f32[]{:T(128)} %bitcast.12, f32[32,8192]{1,0:T(8,128)} %all-gather.4.cloned.1.call-done, f32[256,8192]{1,0:T(8,128)} %exponential_multiply_fusion), kind=kOutput, calls=%fused_computation.19 | convolution fusion | flops 805355456 | bytes 9502980 | tf_op jit(solution)/shard_map/while/body/eval_jaxpr/dot_general | solution.py:42
  109.9 37.1 %all-reduce = (f32[32]{0:T(128)S(1)}, f32[32]{0:T(128)S(1)}) all-reduce(f32[32]{0:T(128)S(1)} %get-tuple-element.39, f32[32]{0:T(128)S(1)} %get-tuple-element.38), channel_id=1, replica_groups=mesh['row'=4,'col'=8] {'row','col'}, use_global_device_ids=true, to_apply=%region_1.0 | all-reduce | flops 64 | bytes 512 | tf_op jit(solution)/shard_map/psum | solution.py:55
  147.0 0.2 multiply_reduce_fusion.4
  147.2 41.5 %psum.44 = f32[32]{0:T(128)S(1)} all-reduce(f32[32]{0:T(128)S(1)} %multiply_reduce_fusion.4), channel_id=1, replica_groups=mesh['row'=4,'col'=8] {'row','col'}, use_global_device_ids=true, to_apply=%region_7.8 | all-reduce | flops 32 | bytes 256 | tf_op jit(solution)/shard_map/psum | solution.py:55
  188.7 0.7 multiply_add_fusion.2
  189.5 0.0 all-gather.8.cloned.1.call-start
  189.5 51.3 %all-gather.6.cloned.1.call-done = f32[32,8192]{1,0:T(8,128)} async-done(((f32[32,256]{1,0:T(8,128)}), f32[32,8192]{1,0:T(8,128)}) %all-gather.6.cloned.1.call-update) | async-done | bytes 1048592 | tf_op jit(solution)/shard_map/all_gather | solution.py:74
  240.8 11.1 %multiply_reduce_fusion.3 = (f32[32]{0:T(128)S(1)}, f32[32,256]{1,0:T(8,128)S(1)}) fusion(f32[32,256]{1,0:T(8,128)} %multiply_add_fusion.2, f32[]{:T(128)} %bitcast.14, f32[32,8192]{1,0:T(8,128)} %all-gather.6.cloned.1.call-done, f32[256,8192]{1,0:T(8,128)} %exponential_multiply_fusion), kind=kOutput, calls=%fused_computation.15 | convolution fusion | flops 805339136 | bytes 9502852 | tf_op jit(solution)/shard_map/while/body/eval_jaxpr/dot_general | solution.py:42
  251.9 40.3 %psum.45 = f32[32]{0:T(128)S(1)} all-reduce(f32[32]{0:T(128)S(1)} %get-tuple-element.61), channel_id=1, replica_groups=mesh['row'=4,'col'=8] {'row','col'}, use_global_device_ids=true, to_apply=%region_9.10 | all-reduce | flops 32 | bytes 256 | tf_op jit(solution)/shard_map/psum | solution.py:77
  292.1 0.2 multiply_reduce_fusion.2
  292.3 39.2 %psum.46 = f32[32]{0:T(128)S(1)} all-reduce(f32[32]{0:T(128)S(1)} %get-tuple-element.48), channel_id=1, replica_groups=mesh['row'=4,'col'=8] {'row','col'}, use_global_device_ids=true, to_apply=%region_11.12 | all-reduce | flops 32 | bytes 256 | tf_op jit(solution)/shard_map/psum | solution.py:55
  331.5 0.7 multiply_add_fusion.1
  332.3 52.0 %all-gather.8.cloned.1.call-done = f32[32,8192]{1,0:T(8,128)} async-done(((f32[32,256]{1,0:T(8,128)}), f32[32,8192]{1,0:T(8,128)}) %all-gather.8.cloned.1.call-update) | async-done | bytes 1048592 | tf_op jit(solution)/shard_map/all_gather | solution.py:74
  384.2 11.1 %multiply_reduce_fusion.1 = (f32[32]{0:T(128)S(1)}, f32[32,256]{1,0:T(8,128)S(1)}) fusion(f32[32,256]{1,0:T(8,128)} %multiply_add_fusion.1, f32[]{:T(128)} %bitcast.13, f32[32,8192]{1,0:T(8,128)} %all-gather.8.cloned.1.call-done, f32[256,8192]{1,0:T(8,128)} %exponential_multiply_fusion), kind=kOutput, calls=%fused_computation.11 | convolution fusion | flops 805339136 | bytes 9502852 | tf_op jit(solution)/shard_map/while/body/eval_jaxpr/dot_general | solution.py:42
  395.3 40.3 %psum.47 = f32[32]{0:T(128)S(1)} all-reduce(f32[32]{0:T(128)S(1)} %get-tuple-element.63), channel_id=1, replica_groups=mesh['row'=4,'col'=8] {'row','col'}, use_global_device_ids=true, to_apply=%region_13.14 | all-reduce | flops 32 | bytes 256 | tf_op jit(solution)/shard_map/psum | solution.py:77
  435.5 0.7 multiply_subtract_fusion
  (17 shorter events, 0.1 us)
Async XLA Ops:
  7.2 91.6 %all-gather.4.cloned.1.call-start = ((), (), s32[]{:S(2)}) async-start(), calls=%async_computation | async-start | bytes 1081344 | tf_op jit(solution)/shard_map/all_gather | solution.py:74
  9.3 231.5 %all-gather.6.cloned.1.call-start = ((), (), s32[]{:S(2)}) async-start(), calls=%async_computation.1 | async-start | bytes 1081344 | tf_op jit(solution)/shard_map/all_gather | solution.py:74
  84.7 14.0 %copy-start.2 = (f32[32,256]{1,0:T(8,128)S(1)}, f32[32,256]{1,0:T(8,128)}, u32[]{:S(2)}) copy-start(f32[32,256]{1,0:T(8,128)} %pad_maximum_fusion) | copy-start | bytes 98308
  98.7 48.3 %copy-start.3 = (f32[256]{0:T(256)S(1)}, f32[256]{0:T(256)}, u32[]{:S(2)}) copy-start(f32[256]{0:T(256)} %param.10) | copy-start | bytes 3076
  189.4 142.1 %copy-start = (f32[32,256]{1,0:T(8,128)S(1)}, f32[32,256]{1,0:T(8,128)}, u32[]{:S(2)}) copy-start(f32[32,256]{1,0:T(8,128)} %multiply_add_fusion.2) | copy-start | bytes 98308
  189.5 194.7 %all-gather.8.cloned.1.call-start = ((), (), s32[]{:S(2)}) async-start(), calls=%async_computation.2 | async-start | bytes 1081344 | tf_op jit(solution)/shard_map/all_gather | solution.py:74
  332.2 103.3 %copy-start.1 = (f32[32,256]{1,0:T(8,128)S(1)}, f32[32,256]{1,0:T(8,128)}, u32[]{:S(2)}) copy-start(f32[32,256]{1,0:T(8,128)} %multiply_add_fusion.1) | copy-start | bytes 98308
Sparse Core Ops, SparseCore 0:
  11.4 54.6 all-gather.3
  189.6 51.1 all-gather.5
  332.4 51.7 all-gather.7
where the time goes:
time: 444 us; the launch traced here: 443 us
  blocking collectives  272 us (61%)
  waiting for transfers between devices  103 us (23%)
  matrix products  47.3 us (11%)
  between operations  15.1 us (3%)
  other arithmetic  5.46 us (1%)
    psum x3, blocking collectives, squares(): return lax.psum(jnp.sum(residual * residual, axis=1), ('row', 'col'))  118 us
    all_gather x3, waiting for transfers between devices, body(): lax.all_gather(direction, ('row', 'col'), axis=1, tiled=True)  103 us
    psum x2, blocking collectives, body(): curved = lax.psum(jnp.sum(direction * image, axis=1), ('row', 'col'))  80.5 us
    all_gather x1, blocking collectives, body(): every_point = lax.all_gather(scaled, ('row', 'col'), axis=1, tiled=True)  73.2 us
    dot_general x3, matrix products, one_block(): lax.dot_general(vectors, kernel_tile, (((1,), (1,)), ((), ())), precision...  33.3 us
    dot_general x1, matrix products, matern_tile(): lax.dot_general(row_scaled, col_scaled, (((0,), (0,)), ((), ())), precisi...  14 us
  transfers between devices with their start and end apart: 3, of which 2 were waited for; matrix products, arithmetic and copies ran while one was open for 3% of the time, Pallas kernels for 0%

commit v1 on v0

--- a/solution.py
+++ b/solution.py
@@ -71,7 +71,12 @@
             scaled,
             every_point,
             signal_value,
-            lax.all_gather(direction, ("row", "col"), axis=1, tiled=True),
+            jnp.concatenate(
+                lax.all_to_all(
+                    jnp.stack([direction] * lax.axis_size(("row", "col"))), ("row", "col"), 0, 0
+                ),
+                axis=1,
+            ),
         )
         image = summed + noise_value * direction
         curved = lax.psum(jnp.sum(direction * image, axis=1), ("row", "col"))

time: 444 us -> 400 us (0.901)
  waiting for transfers between devices: 103 us -> 0.01 us
  blocking collectives: 272 us -> 341 us
  between operations: 15.1 us -> 2 us
  starting transfers between devices: 0.12 us -> 7.33 us
    all_gather x3 -> x0, waiting for transfers between devices: 103 us -> none  [body(): lax.all_gather(direction, ('row', 'col'), axis=1, tiled=True)]
    all_to_all x0 -> x2, blocking collectives: none -> 63 us  [body(): lax.all_to_all(jnp.stack([direction] * lax.axis_size(('row', 'col'))), ('...]
    all_gather x1, blocking collectives: 73.2 us -> 82.9 us  [body(): every_point = lax.all_gather(scaled, ('row', 'col'), axis=1, tiled=True)]
    all_to_all x0 -> x1, starting transfers between devices: none -> 7.33 us  [body(): lax.all_to_all(jnp.stack([direction] * lax.axis_size(('row', 'col'))), ('...]
    psum x2, blocking collectives: 80.5 us -> 75.9 us  [body(): curved = lax.psum(jnp.sum(direction * image, axis=1), ('row', 'col'))]
  transfers between devices with their start and end apart: 3 -> 1, of which waited for: 2 -> 0; matrix products, arithmetic and copies ran while one was open for 3% -> 4% of each run, Pallas kernels for 0% -> 0%
where the time goes in v1:
time: 400 us; the launch traced here: 399 us
  blocking collectives  341 us (85%)
  matrix products  43.5 us (11%)
  starting transfers between devices  7.33 us (2%)
    psum x3, blocking collectives, squares(): return lax.psum(jnp.sum(residual * residual, axis=1), ('row', 'col'))  119 us
    all_gather x1, blocking collectives, body(): every_point = lax.all_gather(scaled, ('row', 'col'), axis=1, tiled=True)  82.9 us
    psum x2, blocking collectives, body(): curved = lax.psum(jnp.sum(direction * image, axis=1), ('row', 'col'))  75.9 us
    all_to_all x2, blocking collectives, body(): lax.all_to_all(jnp.stack([direction] * lax.axis_size(('row', 'col'))), ('...  63 us
    dot_general x3, matrix products, one_block(): lax.dot_general(vectors, kernel_tile, (((1,), (1,)), ((), ())), precision...  29.5 us
    dot_general x1, matrix products, matern_tile(): lax.dot_general(row_scaled, col_scaled, (((0,), (0,)), ((), ())), precisi...  14 us
  transfers between devices with their start and end apart: 1, of which 0 were waited for; matrix products, arithmetic and copies ran while one was open for 4% of the time, Pallas kernels for 0%

profile of v1, /device:TPU:0, one launch (start us, length us, event | category | flops | bytes accessed | tf_op | source)
XLA Modules:
  0.0 399.0 jit_solution(8145861089506825722)
XLA Ops:
  0.6 0.8 multiply_add_fusion.3
  1.4 0.7 pad_maximum_fusion
  2.1 1.2 stack.6
  3.3 7.3 %all-to-all-start = ((f32[32,32,256]{2,1,0:T(8,128)}), f32[32,32,256]{2,1,0:T(8,128)S(1)}, u32[]{:S(2)}, u32[]{:S(2)}) async-start(f32[32,32,256]{2,1,0:T(8,128)} %stack.6), calls=%async_computation | async-start | bytes 2097152 | tf_op jit(solution)/shard_map/all_to_all | solution.py:75
  11.9 0.8 multiply_reduce_fusion.7
  12.7 82.9 %all_gather.3 = f32[16,8192]{1,0:T(8,128)S(1)} all-gather(f32[16,256]{1,0:T(8,128)S(1)} %get-tuple-element.51), channel_id=1, replica_groups=mesh['row'=4,'col'=8] {'row','col'}, dimensions={1}, use_global_device_ids=true | all-gather | bytes 540672 | tf_op jit(solution)/shard_map/all_gather | solution.py:64
  95.6 0.1 multiply_reduce_fusion
  95.7 14.0 %exponential_multiply_fusion = f32[256,8192]{1,0:T(8,128)} fusion(f32[16,256]{1,0:T(8,128)S(1)} %get-tuple-element.51, f32[16,8192]{1,0:T(8,128)S(1)} %all_gather.3, f32[8192]{0:T(1024)S(1)} %multiply_reduce_fusion, f32[256]{0:T(256)S(1)} %get-tuple-element.50, f32[]{:T(128)} %bitcast.20), kind=kOutput, calls=%fused_computation.3 | convolution fusion | flops 425721856 | bytes 8963076 | tf_op jit(solution)/shard_map/while/body/eval_jaxpr/dot_general | solution.py:13
  109.8 9.8 %multiply_reduce_fusion.5 = (f32[32]{0:T(128)S(1)}, f32[32]{0:T(128)S(1)}, f32[32,256]{1,0:T(8,128)S(1)}) fusion(f32[32,256]{1,0:T(8,128)S(1)} %pad_maximum_fusion, f32[]{:T(128)} %bitcast.21, f32[32,8192]{1,0:T(8,128)S(1)} %bitcast.24, f32[256,8192]{1,0:T(8,128)} %exponential_multiply_fusion), kind=kOutput, calls=%fused_computation.19 | convolution fusion | flops 805355456 | bytes 9502980 | tf_op jit(solution)/shard_map/while/body/eval_jaxpr/dot_general | solution.py:42
  119.6 36.8 %all-reduce = (f32[32]{0:T(128)S(1)}, f32[32]{0:T(128)S(1)}) all-reduce(f32[32]{0:T(128)S(1)} %get-tuple-element.39, f32[32]{0:T(128)S(1)} %get-tuple-element.38), channel_id=1, replica_groups=mesh['row'=4,'col'=8] {'row','col'}, use_global_device_ids=true, to_apply=%region_1.0 | all-reduce | flops 64 | bytes 512 | tf_op jit(solution)/shard_map/psum | solution.py:55
  156.5 0.2 multiply_reduce_fusion.4
  156.6 41.9 %psum.44 = f32[32]{0:T(128)S(1)} all-reduce(f32[32]{0:T(128)S(1)} %multiply_reduce_fusion.4), channel_id=1, replica_groups=mesh['row'=4,'col'=8] {'row','col'}, use_global_device_ids=true, to_apply=%region_7.8 | all-reduce | flops 32 | bytes 256 | tf_op jit(solution)/shard_map/psum | solution.py:55
  198.5 0.1 multiply_add_fusion.2
  198.6 0.1 stack.7
  198.8 31.3 %all_to_all.15 = f32[32,32,256]{2,1,0:T(8,128)S(1)} all-to-all(f32[32,32,256]{2,1,0:T(8,128)S(1)} %stack.7), channel_id=1, replica_groups=mesh['row'=4,'col'=8] {'row','col'}, dimensions={0} | all-to-all | bytes 2097152 | tf_op jit(solution)/shard_map/all_to_all | solution.py:75
  230.1 9.8 %multiply_reduce_fusion.3 = (f32[32]{0:T(128)S(1)}, f32[32,256]{1,0:T(8,128)S(1)}) fusion(f32[32,256]{1,0:T(8,128)S(1)} %multiply_add_fusion.2, f32[]{:T(128)} %bitcast.23, f32[32,8192]{1,0:T(8,128)S(1)} %bitcast.26, f32[256,8192]{1,0:T(8,128)} %exponential_multiply_fusion), kind=kOutput, calls=%fused_computation.15 | convolution fusion | flops 805339136 | bytes 9502852 | tf_op jit(solution)/shard_map/while/body/eval_jaxpr/dot_general | solution.py:42
  240.0 38.0 %psum.45 = f32[32]{0:T(128)S(1)} all-reduce(f32[32]{0:T(128)S(1)} %get-tuple-element.61), channel_id=1, replica_groups=mesh['row'=4,'col'=8] {'row','col'}, use_global_device_ids=true, to_apply=%region_9.10 | all-reduce | flops 32 | bytes 256 | tf_op jit(solution)/shard_map/psum | solution.py:82
  277.9 0.2 multiply_reduce_fusion.2
  278.1 40.4 %psum.46 = f32[32]{0:T(128)S(1)} all-reduce(f32[32]{0:T(128)S(1)} %get-tuple-element.48), channel_id=1, replica_groups=mesh['row'=4,'col'=8] {'row','col'}, use_global_device_ids=true, to_apply=%region_11.12 | all-reduce | flops 32 | bytes 256 | tf_op jit(solution)/shard_map/psum | solution.py:55
  318.6 0.1 stack.8
  318.8 31.7 %all_to_all.16 = f32[32,32,256]{2,1,0:T(8,128)S(1)} all-to-all(f32[32,32,256]{2,1,0:T(8,128)S(1)} %stack.8), channel_id=1, replica_groups=mesh['row'=4,'col'=8] {'row','col'}, dimensions={0} | all-to-all | bytes 2097152 | tf_op jit(solution)/shard_map/all_to_all | solution.py:75
  350.5 9.8 %multiply_reduce_fusion.1 = (f32[32]{0:T(128)S(1)}, f32[32,256]{1,0:T(8,128)S(1)}) fusion(f32[32,256]{1,0:T(8,128)S(1)} %multiply_add_fusion.1, f32[]{:T(128)} %bitcast.22, f32[32,8192]{1,0:T(8,128)S(1)} %bitcast.25, f32[256,8192]{1,0:T(8,128)} %exponential_multiply_fusion), kind=kOutput, calls=%fused_computation.11 | convolution fusion | flops 805339136 | bytes 9502852 | tf_op jit(solution)/shard_map/while/body/eval_jaxpr/dot_general | solution.py:42
  360.3 38.0 %psum.47 = f32[32]{0:T(128)S(1)} all-reduce(f32[32]{0:T(128)S(1)} %get-tuple-element.63), channel_id=1, replica_groups=mesh['row'=4,'col'=8] {'row','col'}, use_global_device_ids=true, to_apply=%region_13.14 | all-reduce | flops 32 | bytes 256 | tf_op jit(solution)/shard_map/psum | solution.py:82
  398.3 0.7 multiply_subtract_fusion
  (12 shorter events, 0.3 us)
Async XLA Ops:
  3.3 106.4 %all-to-all-start = ((f32[32,32,256]{2,1,0:T(8,128)}), f32[32,32,256]{2,1,0:T(8,128)S(1)}, u32[]{:S(2)}, u32[]{:S(2)}) async-start(f32[32,32,256]{2,1,0:T(8,128)} %stack.6), calls=%async_computation | async-start | bytes 2097152 | tf_op jit(solution)/shard_map/all_to_all | solution.py:75
  109.7 46.8 %copy-start = (f32[256]{0:T(256)S(1)}, f32[256]{0:T(256)}, u32[]{:S(2)}) copy-start(f32[256]{0:T(256)} %param.10) | copy-start | bytes 3076
